TPU v7x, 256 devices: a whole 4x4x8 slice. The times are simulated.
256 devices in a mesh: row: 8 (over y, core), col: 32 (over x, z).
Axes of the slice: x: 4, y: 4, z: 8, core: 2. Of those that a mesh axis runs over, the one named last changes fastest.
Arguments:
- x_blocks: bfloat16 [8, 32, 42, 128, 128], P('row', 'col'), may hold values from -1.1953125 to 1.1953125
- x_slots: int32 [8, 32, 42], replicated, may hold values from 0 to 255, as said below
- x_count: int32 [8, 32], replicated, may hold values from 21 to 42, as said below
- s_slots: int32 [8, 32, 2], replicated, may hold values from 0 to 15, as said below
- s_count: int32 [8, 32], replicated, may hold values from 1 to 2, as said below
Outputs:
- square_blocks: bfloat16 [8, 32, 2, 128, 128], P('row', 'col')
- result_blocks: bfloat16 [8, 32, 2, 128, 128], P('row', 'col')
Inputs may be any that keep to these rules, and one draw needn't show every extreme that they name: `x_slots`: in each tile the live slots hold distinct positions; the live blocks whose position % 32 is below 2 come first among the live slots, at most 2 of them, and some tile has exactly 2. Positions of slots that are not live are arbitrary within the range. `x_count`: some tile has exactly 42 live slots. `s_slots`: in each tile the live slots hold distinct positions. `s_count`: some tile has exactly 2 live slots.
All inputs are finite; a program needn't handle non-finite values.
Results may differ from a plain program's by a relative error of at most 0.0049.
Values may be sent and summed in bfloat16 or wider, within the bound.
A program may use at most 128 MiB of HBM per device.

v0:
```python
import math
import jax
import jax.numpy as jnp
from jax import lax
from jax.sharding import PartitionSpec as P

RB = 8
JW = 2
CAPW = 2


def laid_out(pieces, dim):
    dims = list(pieces.shape[1:])
    dims[dim] *= pieces.shape[0]
    return jnp.moveaxis(pieces, 0, dim).reshape(dims)


def copy_for_each(array, axis):
    length = lax.axis_size(axis)
    return lax.all_to_all(
        jnp.broadcast_to(array[None], (length, *array.shape)), axis, 0, 0, tiled=True
    )


def gathered_copies(array, axis, dim):
    return laid_out(copy_for_each(array, axis), dim)


def match_index(targets, slot_keys, slot_live):
    matches = (targets[..., None] == slot_keys) & slot_live
    ordinal = jnp.arange(1, slot_keys.shape[0] + 1, dtype=jnp.int32)
    located = jnp.sum(jnp.where(matches, ordinal, 0), axis=-1)
    return jnp.where(located > 0, located - 1, slot_keys.shape[0])


def local(x_blocks, x_slots, x_count, s_slots, s_count):
    row_total = lax.axis_size("row")
    col_total = lax.axis_size("col")
    row_id = lax.axis_index("row")
    col_id = lax.axis_index("col")
    capacity = x_blocks.shape[2]
    block_size = x_blocks.shape[3]
    order_blocks = RB * col_total
    tile_width = order_blocks // row_total
    panel_all = lax.all_gather(x_blocks, "row", axis=0, tiled=True)
    stacked = panel_all.reshape(row_total * capacity, block_size, block_size)
    padded = jnp.concatenate(
        [stacked, jnp.zeros((1, block_size, block_size), stacked.dtype)], axis=0
    )
    column_slots = lax.dynamic_index_in_dim(x_slots, col_id, 1, keepdims=False)
    column_count = lax.dynamic_index_in_dim(x_count, col_id, 1, keepdims=False)
    ordinal = jnp.arange(capacity, dtype=jnp.int32)
    panel_live = (ordinal[None, :] < column_count[:, None]).reshape(-1)
    owners = jnp.arange(row_total, dtype=jnp.int32)[:, None]
    panel_keys = (
        column_slots // tile_width * order_blocks + owners * tile_width + column_slots % tile_width
    ).reshape(-1)
    row_lanes = jnp.arange(RB, dtype=jnp.int32)
    window_ids = jnp.arange(JW, dtype=jnp.int32)

    def accumulate(running, values, inner_row, inner_col, usable):
        picked = match_index(
            row_lanes[None, :] * order_blocks + inner_row[:, None], panel_keys, panel_live
        )
        left_part = jnp.take(padded, picked, axis=0)
        placing = ((inner_col[:, None] == window_ids[None, :]) & usable[:, None]).astype(
            values.dtype
        )
        placed = placing[:, :, None, None] * values[:, None, :, :]
        return running + jnp.einsum(
            "nrxy,njyz->rjxz", left_part, placed, preferred_element_type=jnp.float32
        )

    def make_step(slot_table, count_row, stride, column_limit):

        def fold_step(running, piece, offset):
            pieces = piece.shape[1]
            slot_count = piece.shape[2]
            positions = lax.dynamic_slice_in_dim(slot_table, offset, pieces, 0)[:, :slot_count]
            counts = lax.dynamic_slice_in_dim(count_row, offset, pieces, 0)
            owner_ids = offset + jnp.arange(pieces, dtype=jnp.int32)[:, None]
            inner_row = owner_ids * RB + positions // stride
            inner_col = positions % stride
            usable = (jnp.arange(slot_count, dtype=jnp.int32)[None, :] < counts[:, None]) & (
                inner_col < column_limit
            )
            values = piece.reshape(pieces * slot_count, block_size, block_size)
            return accumulate(
                running, values, inner_row.reshape(-1), inner_col.reshape(-1), usable.reshape(-1)
            )

        return fold_step

    blank_sum = jnp.zeros((RB, JW, block_size, block_size), jnp.float32)

    def collect_all(gathered, fold_step):
        per_turn = math.gcd(col_total, 8)

        def advance(turn_index, running):
            offset = turn_index * per_turn
            portion = lax.dynamic_slice_in_dim(gathered, offset, per_turn, 1)
            return fold_step(running, portion, offset)

        return lax.fori_loop(0, col_total // per_turn, advance, blank_sum)

    row_slots = lax.dynamic_index_in_dim(x_slots, row_id, 0, keepdims=False)
    row_count = lax.dynamic_index_in_dim(x_count, row_id, 0, keepdims=False)
    square_slots = lax.dynamic_index_in_dim(s_slots, row_id, 0, keepdims=False)
    square_count = lax.dynamic_index_in_dim(s_count, row_id, 0, keepdims=False)
    window_part = x_blocks[:, :, :CAPW]
    first_step = make_step(row_slots, row_count, tile_width, JW)
    product = collect_all(gathered_copies(window_part, "col", 1), first_step)
    own_slots = lax.dynamic_index_in_dim(square_slots, col_id, 0, keepdims=False)
    own_count = lax.dynamic_index_in_dim(square_count, col_id, 0, keepdims=False)
    own_live = jnp.arange(own_slots.shape[0], dtype=jnp.int32) < own_count
    flat_one = product.reshape(RB * JW, block_size, block_size)
    square_part = jnp.where(
        own_live[:, None, None], jnp.take(flat_one, own_slots, axis=0), 0.0
    ).astype(jnp.bfloat16)
    square_part = square_part[None, None]
    second_step = make_step(square_slots, square_count, JW, JW)
    second = collect_all(gathered_copies(square_part, "col", 1), second_step)
    own_keys = own_slots // JW * order_blocks + row_id * tile_width + own_slots % JW
    own_block = jnp.take(padded, match_index(own_keys, panel_keys, panel_live), axis=0).astype(
        jnp.float32
    )
    flat_two = second.reshape(RB * JW, block_size, block_size)
    combined = 1.5 * own_block - 0.5 * jnp.take(flat_two, own_slots, axis=0)
    result = jnp.where(own_live[:, None, None], combined, 0.0).astype(jnp.bfloat16)
    return (square_part, result[None, None])


def solution(mesh):
    in_specs = (P("row", "col", None, None, None), P(), P(), P(), P())
    out_specs = (P("row", "col", None, None, None), P("row", "col", None, None, None))
    return jax.shard_map(local, mesh=mesh, in_specs=in_specs, out_specs=out_specs, check_vma=False)
```

profile of v0, /device:TPU:1, one launch (start us, length us, event | category | flops | bytes accessed | tf_op | source)
XLA Modules:
  0.0 268.8 jit_solution(12169378988364675214)
XLA Ops:
  7.2 0.7 all-gather.2.cloned.1.call-update
  7.9 0.8 slice_bitcast_fusion
  8.8 0.1 copy.36
  8.9 1.9 broadcast_in_dim.199
  10.8 11.9 %all-to-all-start = ((bf16[32,1,1,2,128,128]{4,5,3,2,1,0:T(8,128)(2,1)}), bf16[32,1,1,2,128,128]{4,5,3,2,1,0:T(8,128)(2,1)S(1)}, u32[]{:S(2)}, u32[]{:S(2)}) async-start(bf16[32,1,1,2,128,128]{4,5,3,2,1,0:T(8,128)(2,1)} %broadcast_in_dim.199), calls=%async_computation | async-start | bytes 4194304 | tf_op jit(solution)/shard_map/all_to_all | solution.py:20
  22.7 0.5 broadcast.805
  23.2 1.4 fusion.74
  24.8 0.2 dynamic-slice_reduce_fusion
  25.2 0.1 lt.260
  25.4 0.2 fusion.68
  25.5 1.3 dynamic_slice.97
  26.8 0.6 iota_compare_fusion.5
  27.4 0.7 dynamic-slice_bitcast_fusion
  28.2 0.2 fusion.62
  28.4 48.9 %all-gather.2.cloned.1.call-done = bf16[8,1,42,128,128]{4,3,2,1,0:T(8,128)(2,1)} async-done(((bf16[1,1,42,128,128]{4,3,2,1,0:T(8,128)(2,1)}), bf16[8,1,42,128,128]{4,3,2,1,0:T(8,128)(2,1)}) %all-gather.2.cloned.1.call-update) | async-done | bytes 11010064 | tf_op jit(solution)/shard_map/all_gather | solution.py:45
  77.3 10.6 %concatenate.3 = bf16[337,128,128]{2,1,0:T(8,128)(2,1)} pad(bf16[336,128,128]{2,1,0:T(8,128)(2,1)} %bitcast.101, bf16[]{:T(256)} %constant.410.clone.1), padding=0_1x0_0x0_0 | pad | bytes 22052866 | tf_op jit(solution)/shard_map/concatenate | solution.py:47
  87.9 54.0 %while.36 = (s32[]{:T(128)}, f32[8,2,128,128]{2,3,0,1:T(8,128)}, s32[32,42]{1,0:T(8,128)S(1)}, s32[32]{0:T(128)S(1)}, bf16[1,32,2,128,128]{3,4,2,1,0:T(8,128)(2,...) while((s32[]{:T(128)}, f32[8,2,128,128]{2,3,0,1:T(8,128)}, ...), condition=%wide.wide.region_2.4_spmd.clone, body=%wide.wide.region_0.3_spmd.clone.sunk | while | flops 1078636672 | bytes 16272037 | solution.py:104
  88.4 0.1 and.414
  88.5 0.4 select_reduce_fusion.6
  89.0 7.3 %gather_fusion = bf16[128,128,128]{2,1,0:T(8,128)(2,1)} fusion(bf16[337,128,128]{2,1,0:T(8,128)(2,1)} %get-tuple-element.924, s32[1024]{0:T(1024)S(1)} %pad_clamp_fusion.8), kind=kCustom, calls=%fused_computation.clone.clone.clone.1 | custom fusion | bytes 8389120 | tf_op jit(solution)/shard_map/while/body/eval_jaxpr/jit(_take)/gather | solution.py:65
  96.4 0.1 and.415
  96.6 4.6 %fusion.100 = f32[8,2,128,128]{2,3,0,1:T(8,128)} fusion(bf16[16,8,128,128]{3,2,1,0:T(8,128)(2,1)} %bitcast.97, pred[16,8]{0,1:T(8,128)(4,1)S(1)} %copy.73, f32[8,2,128,128]{2,3,0,1:T(8,128)} %get-tuple-element.906, bf16[16,128,128]{1,2,0:T(8,128)(2,1)S(1)} %bitcast.99, bf16[16,2]{0,1:T(2,128)(2,1)S(1)} %and_convert_fusion.6, pred[]{:T(512)S(6)} %compare.58), kind=kOutput, calls=%fused_computation.17.clone.clone.1 | convolution fusion | flops 1078460416 | bytes 6815937 | tf_op jit(solution)/shard_map/while/body/eval_jaxpr/nrxy,njyz->rjxz/dot_general | solution.py:70
  101.7 0.1 and.414
  101.8 0.4 select_reduce_fusion.6
  102.3 7.3 %gather_fusion = bf16[128,128,128]{2,1,0:T(8,128)(2,1)} fusion(bf16[337,128,128]{2,1,0:T(8,128)(2,1)} %get-tuple-element.924, s32[1024]{0:T(1024)S(1)} %pad_clamp_fusion.8), kind=kCustom, calls=%fused_computation.clone.clone.clone.1 | custom fusion | bytes 8389120 | tf_op jit(solution)/shard_map/while/body/eval_jaxpr/jit(_take)/gather | solution.py:65
  109.7 0.1 and.415
  109.9 4.8 %fusion.100 = f32[8,2,128,128]{2,3,0,1:T(8,128)} fusion(bf16[16,8,128,128]{3,2,1,0:T(8,128)(2,1)} %bitcast.97, pred[16,8]{0,1:T(8,128)(4,1)S(1)} %copy.73, f32[8,2,128,128]{2,3,0,1:T(8,128)} %get-tuple-element.906, bf16[16,128,128]{1,2,0:T(8,128)(2,1)S(1)} %bitcast.99, bf16[16,2]{0,1:T(2,128)(2,1)S(1)} %and_convert_fusion.6, pred[]{:T(512)S(6)} %compare.58), kind=kOutput, calls=%fused_computation.17.clone.clone.1 | convolution fusion | flops 1078460416 | bytes 6815937 | tf_op jit(solution)/shard_map/while/body/eval_jaxpr/nrxy,njyz->rjxz/dot_general | solution.py:70
  115.3 0.4 select_reduce_fusion.6
  115.9 7.3 %gather_fusion = bf16[128,128,128]{2,1,0:T(8,128)(2,1)} fusion(bf16[337,128,128]{2,1,0:T(8,128)(2,1)} %get-tuple-element.924, s32[1024]{0:T(1024)S(1)} %pad_clamp_fusion.8), kind=kCustom, calls=%fused_computation.clone.clone.clone.1 | custom fusion | bytes 8389120 | tf_op jit(solution)/shard_map/while/body/eval_jaxpr/jit(_take)/gather | solution.py:65
  123.2 0.1 and.415
  123.5 4.8 %fusion.100 = f32[8,2,128,128]{2,3,0,1:T(8,128)} fusion(bf16[16,8,128,128]{3,2,1,0:T(8,128)(2,1)} %bitcast.97, pred[16,8]{0,1:T(8,128)(4,1)S(1)} %copy.73, f32[8,2,128,128]{2,3,0,1:T(8,128)} %get-tuple-element.906, bf16[16,128,128]{1,2,0:T(8,128)(2,1)S(1)} %bitcast.99, bf16[16,2]{0,1:T(2,128)(2,1)S(1)} %and_convert_fusion.6, pred[]{:T(512)S(6)} %compare.58), kind=kOutput, calls=%fused_computation.17.clone.clone.1 | convolution fusion | flops 1078460416 | bytes 6815937 | tf_op jit(solution)/shard_map/while/body/eval_jaxpr/nrxy,njyz->rjxz/dot_general | solution.py:70
  128.9 0.4 select_reduce_fusion.6
  129.4 7.3 %gather_fusion = bf16[128,128,128]{2,1,0:T(8,128)(2,1)} fusion(bf16[337,128,128]{2,1,0:T(8,128)(2,1)} %get-tuple-element.924, s32[1024]{0:T(1024)S(1)} %pad_clamp_fusion.8), kind=kCustom, calls=%fused_computation.clone.clone.clone.1 | custom fusion | bytes 8389120 | tf_op jit(solution)/shard_map/while/body/eval_jaxpr/jit(_take)/gather | solution.py:65
  137.0 4.8 %fusion.100 = f32[8,2,128,128]{2,3,0,1:T(8,128)} fusion(bf16[16,8,128,128]{3,2,1,0:T(8,128)(2,1)} %bitcast.97, pred[16,8]{0,1:T(8,128)(4,1)S(1)} %copy.73, f32[8,2,128,128]{2,3,0,1:T(8,128)} %get-tuple-element.906, bf16[16,128,128]{1,2,0:T(8,128)(2,1)S(1)} %bitcast.99, bf16[16,2]{0,1:T(2,128)(2,1)S(1)} %and_convert_fusion.6, pred[]{:T(512)S(6)} %compare.58), kind=kOutput, calls=%fused_computation.17.clone.clone.1 | convolution fusion | flops 1078460416 | bytes 6815937 | tf_op jit(solution)/shard_map/while/body/eval_jaxpr/nrxy,njyz->rjxz/dot_general | solution.py:70
  141.9 1.5 copy.37
  143.4 0.6 gather_fusion.3
  144.0 0.1 fusion.53
  144.1 0.1 copy.38
  144.2 1.9 broadcast_in_dim.207
  146.0 9.6 %all-to-all-start.1 = ((bf16[32,1,1,2,128,128]{4,5,3,2,1,0:T(8,128)(2,1)}), bf16[32,1,1,2,128,128]{4,5,3,2,1,0:T(8,128)(2,1)S(1)}, u32[]{:S(2)}, u32[]{:S(2)}) async-start(bf16[32,1,1,2,128,128]{4,5,3,2,1,0:T(8,128)(2,1)} %broadcast_in_dim.207), calls=%async_computation.1 | async-start | bytes 4194304 | tf_op jit(solution)/shard_map/all_to_all | solution.py:20
  155.7 0.7 fusion.72
  156.4 4.7 %gather_fusion.2 = bf16[2,128,128]{2,1,0:T(8,128)(2,1)S(1)} fusion(bf16[337,128,128]{2,1,0:T(8,128)(2,1)} %get-tuple-element.971, s32[1024]{0:T(1024)S(1)} %pad_clamp_fusion.2), kind=kCustom, calls=%fused_computation.4 | custom fusion | bytes 131080 | tf_op jit(solution)/shard_map/jit(_take)/gather | solution.py:124
  161.1 0.7 fusion.75
  161.8 42.7 %all-to-all-done.1 = bf16[32,1,1,2,128,128]{4,5,3,2,1,0:T(8,128)(2,1)S(1)} async-done(((bf16[32,1,1,2,128,128]{4,5,3,2,1,0:T(8,128)(2,1)}), bf16[32,1,1,2,128,128]{4,5,3,2,1,0:T(8,128)(2,1)S(1)}, u32[]{:S(2)}, u32[]{:S(2)}) %all-to-all-start.1) | async-done | bytes 2097184 | tf_op jit(solution)/shard_map/all_to_all | solution.py:20
  204.5 54.6 %while.37 = (s32[]{:T(128)}, f32[8,2,128,128]{2,3,0,1:T(8,128)}, s32[32,2]{0,1:T(2,128)S(1)}, s32[32]{0:T(128)S(1)}, bf16[1,32,2,128,128]{3,4,2,1,0:T(8,128)(2,1...) while((s32[]{:T(128)}, f32[8,2,128,128]{2,3,0,1:T(8,128)}, ...), condition=%wide.wide.region_6.9_spmd.clone, body=%wide.wide.region_4.8_spmd.clone.sunk | while | flops 1078636672 | bytes 16269573 | solution.py:104
  204.8 0.1 and.424
  205.4 0.4 select_reduce_fusion.7
  206.0 7.3 %gather_fusion.1 = bf16[128,128,128]{2,1,0:T(8,128)(2,1)} fusion(bf16[337,128,128]{2,1,0:T(8,128)(2,1)} %get-tuple-element.963, s32[1024]{0:T(1024)S(1)} %pad_clamp_fusion.9), kind=kCustom, calls=%fused_computation.2.clone.clone.clone.1 | custom fusion | bytes 8389120 | tf_op jit(solution)/shard_map/while/body/eval_jaxpr/jit(_take)/gather | solution.py:65
  213.4 4.6 %fusion.105 = f32[8,2,128,128]{2,3,0,1:T(8,128)} fusion(bf16[16,8,128,128]{3,2,1,0:T(8,128)(2,1)} %bitcast.98, pred[16,8]{0,1:T(8,128)(4,1)S(1)} %copy.76, f32[8,2,128,128]{2,3,0,1:T(8,128)} %get-tuple-element.945, bf16[16,128,128]{1,2,0:T(8,128)(2,1)S(1)} %bitcast.100, bf16[16,2]{0,1:T(2,128)(2,1)S(1)} %and_convert_fusion.7, pred[]{:T(512)S(6)} %compare.59), kind=kOutput, calls=%fused_computation.53.clone.clone.1 | convolution fusion | flops 1078460416 | bytes 6815937 | tf_op jit(solution)/shard_map/while/body/eval_jaxpr/nrxy,njyz->rjxz/dot_general | solution.py:70
  218.3 0.1 and.424
  218.9 0.4 select_reduce_fusion.7
  219.4 7.3 %gather_fusion.1 = bf16[128,128,128]{2,1,0:T(8,128)(2,1)} fusion(bf16[337,128,128]{2,1,0:T(8,128)(2,1)} %get-tuple-element.963, s32[1024]{0:T(1024)S(1)} %pad_clamp_fusion.9), kind=kCustom, calls=%fused_computation.2.clone.clone.clone.1 | custom fusion | bytes 8389120 | tf_op jit(solution)/shard_map/while/body/eval_jaxpr/jit(_take)/gather | solution.py:65
  226.8 4.8 %fusion.105 = f32[8,2,128,128]{2,3,0,1:T(8,128)} fusion(bf16[16,8,128,128]{3,2,1,0:T(8,128)(2,1)} %bitcast.98, pred[16,8]{0,1:T(8,128)(4,1)S(1)} %copy.76, f32[8,2,128,128]{2,3,0,1:T(8,128)} %get-tuple-element.945, bf16[16,128,128]{1,2,0:T(8,128)(2,1)S(1)} %bitcast.100, bf16[16,2]{0,1:T(2,128)(2,1)S(1)} %and_convert_fusion.7, pred[]{:T(512)S(6)} %compare.59), kind=kOutput, calls=%fused_computation.53.clone.clone.1 | convolution fusion | flops 1078460416 | bytes 6815937 | tf_op jit(solution)/shard_map/while/body/eval_jaxpr/nrxy,njyz->rjxz/dot_general | solution.py:70
  232.0 0.1 and.424
  232.6 0.4 select_reduce_fusion.7
  233.1 7.3 %gather_fusion.1 = bf16[128,128,128]{2,1,0:T(8,128)(2,1)} fusion(bf16[337,128,128]{2,1,0:T(8,128)(2,1)} %get-tuple-element.963, s32[1024]{0:T(1024)S(1)} %pad_clamp_fusion.9), kind=kCustom, calls=%fused_computation.2.clone.clone.clone.1 | custom fusion | bytes 8389120 | tf_op jit(solution)/shard_map/while/body/eval_jaxpr/jit(_take)/gather | solution.py:65
  240.5 4.8 %fusion.105 = f32[8,2,128,128]{2,3,0,1:T(8,128)} fusion(bf16[16,8,128,128]{3,2,1,0:T(8,128)(2,1)} %bitcast.98, pred[16,8]{0,1:T(8,128)(4,1)S(1)} %copy.76, f32[8,2,128,128]{2,3,0,1:T(8,128)} %get-tuple-element.945, bf16[16,128,128]{1,2,0:T(8,128)(2,1)S(1)} %bitcast.100, bf16[16,2]{0,1:T(2,128)(2,1)S(1)} %and_convert_fusion.7, pred[]{:T(512)S(6)} %compare.59), kind=kOutput, calls=%fused_computation.53.clone.clone.1 | convolution fusion | flops 1078460416 | bytes 6815937 | tf_op jit(solution)/shard_map/while/body/eval_jaxpr/nrxy,njyz->rjxz/dot_general | solution.py:70
  245.7 0.1 and.424
  246.3 0.4 select_reduce_fusion.7
  246.8 7.3 %gather_fusion.1 = bf16[128,128,128]{2,1,0:T(8,128)(2,1)} fusion(bf16[337,128,128]{2,1,0:T(8,128)(2,1)} %get-tuple-element.963, s32[1024]{0:T(1024)S(1)} %pad_clamp_fusion.9), kind=kCustom, calls=%fused_computation.2.clone.clone.clone.1 | custom fusion | bytes 8389120 | tf_op jit(solution)/shard_map/while/body/eval_jaxpr/jit(_take)/gather | solution.py:65
  254.2 4.8 %fusion.105 = f32[8,2,128,128]{2,3,0,1:T(8,128)} fusion(bf16[16,8,128,128]{3,2,1,0:T(8,128)(2,1)} %bitcast.98, pred[16,8]{0,1:T(8,128)(4,1)S(1)} %copy.76, f32[8,2,128,128]{2,3,0,1:T(8,128)} %get-tuple-element.945, bf16[16,128,128]{1,2,0:T(8,128)(2,1)S(1)} %bitcast.100, bf16[16,2]{0,1:T(2,128)(2,1)S(1)} %and_convert_fusion.7, pred[]{:T(512)S(6)} %compare.59), kind=kOutput, calls=%fused_computation.53.clone.clone.1 | convolution fusion | flops 1078460416 | bytes 6815937 | tf_op jit(solution)/shard_map/while/body/eval_jaxpr/nrxy,njyz->rjxz/dot_general | solution.py:70
  259.1 1.6 copy.40
  260.7 0.6 gather_fusion.4
  261.2 0.7 fusion.54
  (184 shorter events, 8.2 us)
Async XLA Ops:
  7.2 18.2 %copy-start = (s32[8,32,2]{1,2,0:T(2,128)S(1)}, s32[8,32,2]{1,2,0:T(2,128)}, u32[]{:S(2)}) copy-start(s32[8,32,2]{1,2,0:T(2,128)} %param.16) | copy-start | bytes 6148
  7.2 17.6 %copy-start.3 = (s32[8,32]{1,0:T(8,128)S(1)}, s32[8,32]{1,0:T(8,128)}, u32[]{:S(2)}) copy-start(s32[8,32]{1,0:T(8,128)} %param.15) | copy-start | bytes 3076
  7.2 70.1 %all-gather.2.cloned.1.call-start = ((), (), s32[]{:S(2)}) async-start(), calls=%async_computation.2 | async-start | bytes 12386304 | tf_op jit(solution)/shard_map/all_gather | solution.py:45
  10.8 77.2 %all-to-all-start = ((bf16[32,1,1,2,128,128]{4,5,3,2,1,0:T(8,128)(2,1)}), bf16[32,1,1,2,128,128]{4,5,3,2,1,0:T(8,128)(2,1)S(1)}, u32[]{:S(2)}, u32[]{:S(2)}) async-start(bf16[32,1,1,2,128,128]{4,5,3,2,1,0:T(8,128)(2,1)} %broadcast_in_dim.199), calls=%async_computation | async-start | bytes 4194304 | tf_op jit(solution)/shard_map/all_to_all | solution.py:20
  24.7 63.2 %copy-start.1 = (s32[8,42]{1,0:T(8,128)}, s32[8,42]{1,0:T(8,128)S(1)}, u32[]{:S(2)}) copy-start(s32[8,42]{1,0:T(8,128)S(1)} %fusion.57) | copy-start | bytes 4036
  141.9 13.7 %copy-start.2 = (s32[8,42]{1,0:T(8,128)S(1)}, s32[8,42]{1,0:T(8,128)}, u32[]{:S(2)}) copy-start(s32[8,42]{1,0:T(8,128)} %get-tuple-element.981) | copy-start | bytes 4036
  146.0 58.5 %all-to-all-start.1 = ((bf16[32,1,1,2,128,128]{4,5,3,2,1,0:T(8,128)(2,1)}), bf16[32,1,1,2,128,128]{4,5,3,2,1,0:T(8,128)(2,1)S(1)}, u32[]{:S(2)}, u32[]{:S(2)}) async-start(bf16[32,1,1,2,128,128]{4,5,3,2,1,0:T(8,128)(2,1)} %broadcast_in_dim.207), calls=%async_computation.1 | async-start | bytes 4194304 | tf_op jit(solution)/shard_map/all_to_all | solution.py:20
Sparse Core Ops, SparseCore 0:
  9.8 67.4 all-gather.1
where the time goes:
time: 270 us; the launch traced here: 269 us
  local copies, waits for them, and re-layouts  93.6 us (35%)
  waiting for transfers between devices  92.3 us (34%)
  matrix products  38.2 us (14%)
  starting transfers between devices  21.5 us (8%)
  between operations  14.2 us (5%)
  other arithmetic  8.6 us (3%)
    gather x8, local copies, waits for them, and re-layouts, accumulate(): left_part = jnp.take(padded, picked, axis=0)  58.1 us
    all_gather x1, waiting for transfers between devices, local(): panel_all = lax.all_gather(x_blocks, 'row', axis=0, tiled=True)  48.9 us
    all_to_all x2, waiting for transfers between devices, copy_for_each(): lax.all_to_all(jnp.broadcast_to(array[None], (length, *array.shape)), axi...  42.7 us
    dot_general x8, matrix products, accumulate(): jnp.einsum('nrxy,njyz->rjxz', left_part, placed, preferred_element_type=j...  38.2 us
    all_to_all x2, starting transfers between devices, copy_for_each(): lax.all_to_all(jnp.broadcast_to(array[None], (length, *array.shape)), axi...  21.4 us
    concatenate x1, local copies, waits for them, and re-layouts, local(): jnp.concatenate([stacked, jnp.zeros((1, block_size, block_size), stacked....  10.6 us
  transfers between devices with their start and end apart: 3, of which 2 were waited for; matrix products, arithmetic and copies ran while one was open for 9% of the time, Pallas kernels for 0%

commit v1 on v0

--- a/solution.py
+++ b/solution.py
@@ -7,6 +7,29 @@
 RB = 8
 JW = 2
 CAPW = 2
+
+
+def mix_the_edge(raw, array_dim):
+    x_next, r2, r1 = (lax.psum(1, "row"), lax.axis_index("row"), raw.shape[array_dim])
+    line_up = tuple(((u, (u + 1) % x_next) for u in range(x_next)))
+    panels = tuple(((u, (u - 1) % x_next) for u in range(x_next)))
+    prior = jnp.zeros((*raw.shape[:array_dim], x_next * r1, *raw.shape[array_dim + 1 :]), raw.dtype)
+    prior = lax.dynamic_update_slice_in_dim(prior, raw, r2 * r1, axis=array_dim)
+    k_now = v1 = raw
+    block_last = x_next // 2
+    i0 = 1
+    while i0 < block_last + 1:
+        k_now = lax.ppermute(k_now, "row", line_up)
+        prior = lax.dynamic_update_slice_in_dim(
+            prior, k_now, (r2 - i0) % x_next * r1, axis=array_dim
+        )
+        if i0 < x_next - block_last:
+            v1 = lax.ppermute(v1, "row", perm=panels)
+            prior = lax.dynamic_update_slice_in_dim(
+                prior, v1, (r2 + i0) % x_next * r1, axis=array_dim
+            )
+        i0 += 1
+    return prior
 
 
 def laid_out(pieces, dim):
@@ -42,7 +65,7 @@
     block_size = x_blocks.shape[3]
     order_blocks = RB * col_total
     tile_width = order_blocks // row_total
-    panel_all = lax.all_gather(x_blocks, "row", axis=0, tiled=True)
+    panel_all = mix_the_edge(x_blocks, array_dim=0)
     stacked = panel_all.reshape(row_total * capacity, block_size, block_size)
     padded = jnp.concatenate(
         [stacked, jnp.zeros((1, block_size, block_size), stacked.dtype)], axis=0

time: 270 us -> 256 us (0.948)
  the two profiles are of different devices: /device:TPU:1 before, /device:TPU:27 now
where the time goes in v1:
time: 256 us; the launch traced here: 255 us
  local copies, waits for them, and re-layouts  101 us (39%)
  waiting for transfers between devices  81.2 us (32%)
  matrix products  32.2 us (13%)
  starting transfers between devices  29.4 us (11%)
  other arithmetic  8.69 us (3%)
    gather x8, local copies, waits for them, and re-layouts, accumulate(): left_part = jnp.take(padded, picked, axis=0)  57.3 us
    all_to_all x2, waiting for transfers between devices, copy_for_each(): lax.all_to_all(jnp.broadcast_to(array[None], (length, *array.shape)), axi...  45.3 us
    dot_general x8, matrix products, accumulate(): jnp.einsum('nrxy,njyz->rjxz', left_part, placed, preferred_element_type=j...  32.2 us
    ppermute x3, waiting for transfers between devices, mix_the_edge(): v1 = lax.ppermute(v1, 'row', perm=panels)  20.1 us
    all_to_all x2, starting transfers between devices, copy_for_each(): lax.all_to_all(jnp.broadcast_to(array[None], (length, *array.shape)), axi...  19.2 us
    ppermute x4, waiting for transfers between devices, mix_the_edge(): k_now = lax.ppermute(k_now, 'row', line_up)  15.8 us
    ppermute x4, starting transfers between devices, mix_the_edge(): k_now = lax.ppermute(k_now, 'row', line_up)  10 us
    concatenate x1, local copies, waits for them, and re-layouts, local(): jnp.concatenate([stacked, jnp.zeros((1, block_size, block_size), stacked....  5.13 us
  transfers between devices with their start and end apart: 9, of which 6 were waited for; matrix products, arithmetic and copies ran while one was open for 12% of the time, Pallas kernels for 0%

profile of v1, /device:TPU:27, one launch (start us, length us, event | category | flops | bytes accessed | tf_op | source)
XLA Modules:
  0.0 254.6 jit_solution(3580214955950441831)
XLA Ops:
  0.7 0.5 collective-permute-start
  1.4 15.4 %collective-permute-done = bf16[1,1,42,128,128]{4,3,2,1,0:T(8,128)(2,1)S(1)} collective-permute-done((bf16[1,1,42,128,128]{4,3,2,1,0:T(8,128)(2,1)}, bf16[1,1,42,128,128]{4,3,2,1,0:T(8,128)(2,1)S(1)}, u32[]{:S(2)}, u32[]{:S(2)}) %collective-permute-start) | collective-permute-done | bytes 1376288 | tf_op jit(solution)/shard_map/ppermute | solution.py:22
  16.7 3.6 %collective-permute-start.2 = (bf16[1,1,42,128,128]{4,3,2,1,0:T(8,128)(2,1)S(1)}, bf16[1,1,42,128,128]{4,3,2,1,0:T(8,128)(2,1)}, u32[]{:S(2)}, u32[]{:S(2)}) collective-permute-start(bf16[1,1,42,128,128]{4,3,2,1,0:T(8,128)(2,1)S(1)} %collective-permute-done), channel_id=1, source_target_pairs={{0,32},{32,64},{64,96},{96,128},{128,160},{160,192},{192,224},{224... | collective-permute-start | bytes 4128776 | tf_op jit(solution)/shard_map/ppermute | solution.py:22
  20.3 0.8 slice_bitcast_fusion
  21.3 1.8 broadcast_in_dim.202
  23.1 11.1 %all-to-all-start = ((bf16[32,1,1,2,128,128]{4,5,3,2,1,0:T(8,128)(2,1)}), bf16[32,1,1,2,128,128]{4,5,3,2,1,0:T(8,128)(2,1)}, u32[]{:S(2)}, u32[]{:S(2)}) async-start(bf16[32,1,1,2,128,128]{4,5,3,2,1,0:T(8,128)(2,1)} %broadcast_in_dim.202), calls=%async_computation | async-start | bytes 4194304 | tf_op jit(solution)/shard_map/all_to_all | solution.py:43
  34.8 1.3 dynamic_slice.97
  36.1 0.5 broadcast.812
  36.6 1.4 fusion.74
  38.1 0.7 iota_compare_fusion.5
  38.9 2.9 %collective-permute-start.4 = (bf16[1,1,42,128,128]{4,3,2,1,0:T(8,128)(2,1)}, bf16[1,1,42,128,128]{4,3,2,1,0:T(8,128)(2,1)}, u32[]{:S(2)}, u32[]{:S(2)}) collective-permute-start(bf16[1,1,42,128,128]{4,3,2,1,0:T(8,128)(2,1)} %collective-permute-done.2), channel_id=1, source_target_pairs={{0,32},{32,64},{64,96},{96,128},{128,160},{160,192},{192,224},{224... | collective-permute-start | bytes 4128776 | tf_op jit(solution)/shard_map/ppermute | solution.py:22
  42.2 0.7 dynamic-slice_bitcast_fusion
  43.2 2.8 %broadcast_in_dim.203 = bf16[8,1,42,128,128]{4,3,2,0,1:T(8,128)(2,1)S(1)} broadcast(bf16[]{:T(256)} %constant.452.clone.1), dimensions={} | broadcast | bytes 11010050 | tf_op jit(solution)/shard_map/broadcast_in_dim | solution.py:16
  46.2 11.4 %collective-permute-done.3 = bf16[1,1,42,128,128]{4,3,2,1,0:T(8,128)(2,1)} collective-permute-done((bf16[1,1,42,128,128]{4,3,2,1,0:T(8,128)(2,1)}, bf16[1,1,42,128,128]{4,3,2,1,0:T(8,128)(2,1)}, u32[]{:S(2)}, u32[]{:S(2)}) %collective-permute-start.3) | collective-permute-done | bytes 1376288 | tf_op jit(solution)/shard_map/ppermute | solution.py:27
  57.7 1.6 bitcast_dynamic-update-slice_fusion.6
  59.3 3.0 %collective-permute-start.6 = (bf16[1,1,42,128,128]{4,3,2,1,0:T(8,128)(2,1)}, bf16[1,1,42,128,128]{4,3,2,1,0:T(8,128)(2,1)S(1)}, u32[]{:S(2)}, u32[]{:S(2)}) collective-permute-start(bf16[1,1,42,128,128]{4,3,2,1,0:T(8,128)(2,1)} %collective-permute-done.4), channel_id=1, source_target_pairs={{0,32},{32,64},{64,96},{96,128},{128,160},{160,192},{192,224},{224... | collective-permute-start | bytes 4128776 | tf_op jit(solution)/shard_map/ppermute | solution.py:22
  62.2 1.6 bitcast_dynamic-update-slice_fusion.5
  63.8 1.6 bitcast_dynamic-update-slice_fusion.4
  65.4 1.6 bitcast_dynamic-update-slice_fusion.3
  67.0 1.6 bitcast_dynamic-update-slice_fusion.2
  68.6 8.6 %collective-permute-done.5 = bf16[1,1,42,128,128]{4,3,2,1,0:T(8,128)(2,1)S(1)} collective-permute-done((bf16[1,1,42,128,128]{4,3,2,1,0:T(8,128)(2,1)}, bf16[1,1,42,128,128]{4,3,2,1,0:T(8,128)(2,1)S(1)}, u32[]{:S(2)}, u32[]{:S(2)}) %collective-permute-start.5) | collective-permute-done | bytes 1376288 | tf_op jit(solution)/shard_map/ppermute | solution.py:27
  77.4 0.4 collective-permute-done.6
  78.0 5.1 %concatenate.3 = bf16[337,128,128]{2,1,0:T(8,128)(2,1)} pad(bf16[336,128,128]{2,1,0:T(8,128)(2,1)S(1)} %bitcast.115, bf16[]{:T(256)} %constant.452.clone.1), padding=0_1x0_0x0_0 | pad | bytes 22052866 | tf_op jit(solution)/shard_map/concatenate | solution.py:70
  83.1 1.1 all-to-all-done
  84.2 51.9 %while.36 = (s32[]{:T(128)}, f32[8,2,128,128]{2,3,0,1:T(8,128)S(1)}, s32[32,42]{1,0:T(8,128)S(1)}, s32[32]{0:T(128)S(1)}, bf16[1,32,2,128,128]{3,4,2,1,0:T(8,128...) while((s32[]{:T(128)}, ...), condition=%wide.wide.region_2.4_spmd.clone, body=%wide.wide.region_0.3_spmd.clone.sunk | while | flops 1078636672 | bytes 16272037 | solution.py:127
  84.8 0.4 select_reduce_fusion.6
  85.3 7.2 %gather_fusion = bf16[128,128,128]{2,1,0:T(8,128)(2,1)} fusion(bf16[337,128,128]{2,1,0:T(8,128)(2,1)} %get-tuple-element.924, s32[1024]{0:T(1024)S(1)} %pad_clamp_fusion.8), kind=kCustom, calls=%fused_computation.clone.clone.clone.1 | custom fusion | bytes 8389120 | tf_op jit(solution)/shard_map/while/body/eval_jaxpr/jit(_take)/gather | solution.py:88
  92.8 1.1 constant_dynamic-slice_fusion.19
  93.9 3.3 %fusion.100 = f32[8,2,128,128]{2,3,0,1:T(8,128)S(1)} fusion(bf16[16,8,128,128]{3,2,1,0:T(8,128)(2,1)} %bitcast.113, pred[16,8]{0,1:T(8,128)(4,1)S(1)} %copy.105, f32[8,2,128,128]{2,3,0,1:T(8,128)S(1)} %get-tuple-element.906, bf16[16,128,128]{1,2,0:T(8,128)(2,1)S(1)} %bitcast.116, bf16[16,2]{0,1:T(2,128)(2,1)S(1)} %and_convert_fusion.6, ...), kind=kOutput, calls=%fused_computation.17.clone.clone.1 | convolution fusion | flops 1078460416 | bytes 6815937 | tf_op jit(solution)/shard_map/while/body/eval_jaxpr/nrxy,njyz->rjxz/dot_general | solution.py:93
  97.8 0.4 select_reduce_fusion.6
  98.3 7.2 %gather_fusion = bf16[128,128,128]{2,1,0:T(8,128)(2,1)} fusion(bf16[337,128,128]{2,1,0:T(8,128)(2,1)} %get-tuple-element.924, s32[1024]{0:T(1024)S(1)} %pad_clamp_fusion.8), kind=kCustom, calls=%fused_computation.clone.clone.clone.1 | custom fusion | bytes 8389120 | tf_op jit(solution)/shard_map/while/body/eval_jaxpr/jit(_take)/gather | solution.py:88
  105.8 1.1 constant_dynamic-slice_fusion.19
  106.9 3.3 %fusion.100 = f32[8,2,128,128]{2,3,0,1:T(8,128)S(1)} fusion(bf16[16,8,128,128]{3,2,1,0:T(8,128)(2,1)} %bitcast.113, pred[16,8]{0,1:T(8,128)(4,1)S(1)} %copy.105, f32[8,2,128,128]{2,3,0,1:T(8,128)S(1)} %get-tuple-element.906, bf16[16,128,128]{1,2,0:T(8,128)(2,1)S(1)} %bitcast.116, bf16[16,2]{0,1:T(2,128)(2,1)S(1)} %and_convert_fusion.6, ...), kind=kOutput, calls=%fused_computation.17.clone.clone.1 | convolution fusion | flops 1078460416 | bytes 6815937 | tf_op jit(solution)/shard_map/while/body/eval_jaxpr/nrxy,njyz->rjxz/dot_general | solution.py:93
  110.8 0.4 select_reduce_fusion.6
  111.3 7.2 %gather_fusion = bf16[128,128,128]{2,1,0:T(8,128)(2,1)} fusion(bf16[337,128,128]{2,1,0:T(8,128)(2,1)} %get-tuple-element.924, s32[1024]{0:T(1024)S(1)} %pad_clamp_fusion.8), kind=kCustom, calls=%fused_computation.clone.clone.clone.1 | custom fusion | bytes 8389120 | tf_op jit(solution)/shard_map/while/body/eval_jaxpr/jit(_take)/gather | solution.py:88
  118.8 1.1 constant_dynamic-slice_fusion.19
  119.8 3.3 %fusion.100 = f32[8,2,128,128]{2,3,0,1:T(8,128)S(1)} fusion(bf16[16,8,128,128]{3,2,1,0:T(8,128)(2,1)} %bitcast.113, pred[16,8]{0,1:T(8,128)(4,1)S(1)} %copy.105, f32[8,2,128,128]{2,3,0,1:T(8,128)S(1)} %get-tuple-element.906, bf16[16,128,128]{1,2,0:T(8,128)(2,1)S(1)} %bitcast.116, bf16[16,2]{0,1:T(2,128)(2,1)S(1)} %and_convert_fusion.6, ...), kind=kOutput, calls=%fused_computation.17.clone.clone.1 | convolution fusion | flops 1078460416 | bytes 6815937 | tf_op jit(solution)/shard_map/while/body/eval_jaxpr/nrxy,njyz->rjxz/dot_general | solution.py:93
  123.8 0.4 select_reduce_fusion.6
  124.3 7.2 %gather_fusion = bf16[128,128,128]{2,1,0:T(8,128)(2,1)} fusion(bf16[337,128,128]{2,1,0:T(8,128)(2,1)} %get-tuple-element.924, s32[1024]{0:T(1024)S(1)} %pad_clamp_fusion.8), kind=kCustom, calls=%fused_computation.clone.clone.clone.1 | custom fusion | bytes 8389120 | tf_op jit(solution)/shard_map/while/body/eval_jaxpr/jit(_take)/gather | solution.py:88
  131.7 1.1 constant_dynamic-slice_fusion.19
  132.8 3.3 %fusion.100 = f32[8,2,128,128]{2,3,0,1:T(8,128)S(1)} fusion(bf16[16,8,128,128]{3,2,1,0:T(8,128)(2,1)} %bitcast.113, pred[16,8]{0,1:T(8,128)(4,1)S(1)} %copy.105, f32[8,2,128,128]{2,3,0,1:T(8,128)S(1)} %get-tuple-element.906, bf16[16,128,128]{1,2,0:T(8,128)(2,1)S(1)} %bitcast.116, bf16[16,2]{0,1:T(2,128)(2,1)S(1)} %and_convert_fusion.6, ...), kind=kOutput, calls=%fused_computation.17.clone.clone.1 | convolution fusion | flops 1078460416 | bytes 6815937 | tf_op jit(solution)/shard_map/while/body/eval_jaxpr/nrxy,njyz->rjxz/dot_general | solution.py:93
  136.5 0.6 gather_fusion.3
  137.2 1.9 broadcast_in_dim.211
  139.1 8.1 %all-to-all-start.1 = ((bf16[32,1,1,2,128,128]{4,5,3,2,1,0:T(8,128)(2,1)}), bf16[32,1,1,2,128,128]{4,5,3,2,1,0:T(8,128)(2,1)S(1)}, u32[]{:S(2)}, u32[]{:S(2)}) async-start(bf16[32,1,1,2,128,128]{4,5,3,2,1,0:T(8,128)(2,1)} %broadcast_in_dim.211), calls=%async_computation.1 | async-start | bytes 4194304 | tf_op jit(solution)/shard_map/all_to_all | solution.py:43
  147.3 0.7 fusion.73
  148.0 4.7 %gather_fusion.2 = bf16[2,128,128]{2,1,0:T(8,128)(2,1)S(1)} fusion(bf16[337,128,128]{2,1,0:T(8,128)(2,1)} %get-tuple-element.970, s32[1024]{0:T(1024)S(1)} %pad_clamp_fusion.2), kind=kCustom, calls=%fused_computation.4 | custom fusion | bytes 131080 | tf_op jit(solution)/shard_map/jit(_take)/gather | solution.py:147
  152.7 0.7 fusion.75
  153.4 44.2 %all-to-all-done.1 = bf16[32,1,1,2,128,128]{4,5,3,2,1,0:T(8,128)(2,1)S(1)} async-done(((bf16[32,1,1,2,128,128]{4,5,3,2,1,0:T(8,128)(2,1)}), bf16[32,1,1,2,128,128]{4,5,3,2,1,0:T(8,128)(2,1)S(1)}, u32[]{:S(2)}, u32[]{:S(2)}) %all-to-all-start.1) | async-done | bytes 2097184 | tf_op jit(solution)/shard_map/all_to_all | solution.py:43
  197.7 54.1 %while.37 = (s32[]{:T(128)}, f32[8,2,128,128]{2,3,0,1:T(8,128)}, s32[32,2]{0,1:T(2,128)S(1)}, s32[32]{0:T(128)S(1)}, bf16[1,32,2,128,128]{3,4,2,1,0:T(8,128)(2,1...) while((s32[]{:T(128)}, f32[8,2,128,128]{2,3,0,1:T(8,128)}, ...), condition=%wide.wide.region_6.9_spmd.clone, body=%wide.wide.region_4.8_spmd.clone.sunk | while | flops 1078636672 | bytes 16269573 | solution.py:127
  198.6 0.4 select_reduce_fusion.7
  199.1 7.2 %gather_fusion.1 = bf16[128,128,128]{2,1,0:T(8,128)(2,1)} fusion(bf16[337,128,128]{2,1,0:T(8,128)(2,1)} %get-tuple-element.963, s32[1024]{0:T(1024)S(1)} %pad_clamp_fusion.9), kind=kCustom, calls=%fused_computation.2.clone.clone.clone.1 | custom fusion | bytes 8389120 | tf_op jit(solution)/shard_map/while/body/eval_jaxpr/jit(_take)/gather | solution.py:88
  206.4 4.5 %fusion.105 = f32[8,2,128,128]{2,3,0,1:T(8,128)} fusion(bf16[16,8,128,128]{3,2,1,0:T(8,128)(2,1)} %bitcast.114, pred[16,8]{0,1:T(8,128)(4,1)S(1)} %copy.108, f32[8,2,128,128]{2,3,0,1:T(8,128)} %get-tuple-element.945, bf16[16,128,128]{1,2,0:T(8,128)(2,1)S(1)} %bitcast.117, bf16[16,2]{0,1:T(2,128)(2,1)S(1)} %and_convert_fusion.7, pred[]{:T(512)S(6)} %compare.66), kind=kOutput, calls=%fused_computation.53.clone.clone.1 | convolution fusion | flops 1078460416 | bytes 6815937 | tf_op jit(solution)/shard_map/while/body/eval_jaxpr/nrxy,njyz->rjxz/dot_general | solution.py:93
  211.9 0.4 select_reduce_fusion.7
  212.4 7.2 %gather_fusion.1 = bf16[128,128,128]{2,1,0:T(8,128)(2,1)} fusion(bf16[337,128,128]{2,1,0:T(8,128)(2,1)} %get-tuple-element.963, s32[1024]{0:T(1024)S(1)} %pad_clamp_fusion.9), kind=kCustom, calls=%fused_computation.2.clone.clone.clone.1 | custom fusion | bytes 8389120 | tf_op jit(solution)/shard_map/while/body/eval_jaxpr/jit(_take)/gather | solution.py:88
  219.7 4.8 %fusion.105 = f32[8,2,128,128]{2,3,0,1:T(8,128)} fusion(bf16[16,8,128,128]{3,2,1,0:T(8,128)(2,1)} %bitcast.114, pred[16,8]{0,1:T(8,128)(4,1)S(1)} %copy.108, f32[8,2,128,128]{2,3,0,1:T(8,128)} %get-tuple-element.945, bf16[16,128,128]{1,2,0:T(8,128)(2,1)S(1)} %bitcast.117, bf16[16,2]{0,1:T(2,128)(2,1)S(1)} %and_convert_fusion.7, pred[]{:T(512)S(6)} %compare.66), kind=kOutput, calls=%fused_computation.53.clone.clone.1 | convolution fusion | flops 1078460416 | bytes 6815937 | tf_op jit(solution)/shard_map/while/body/eval_jaxpr/nrxy,njyz->rjxz/dot_general | solution.py:93
  225.4 0.4 select_reduce_fusion.7
  226.0 7.2 %gather_fusion.1 = bf16[128,128,128]{2,1,0:T(8,128)(2,1)} fusion(bf16[337,128,128]{2,1,0:T(8,128)(2,1)} %get-tuple-element.963, s32[1024]{0:T(1024)S(1)} %pad_clamp_fusion.9), kind=kCustom, calls=%fused_computation.2.clone.clone.clone.1 | custom fusion | bytes 8389120 | tf_op jit(solution)/shard_map/while/body/eval_jaxpr/jit(_take)/gather | solution.py:88
  233.3 4.8 %fusion.105 = f32[8,2,128,128]{2,3,0,1:T(8,128)} fusion(bf16[16,8,128,128]{3,2,1,0:T(8,128)(2,1)} %bitcast.114, pred[16,8]{0,1:T(8,128)(4,1)S(1)} %copy.108, f32[8,2,128,128]{2,3,0,1:T(8,128)} %get-tuple-element.945, bf16[16,128,128]{1,2,0:T(8,128)(2,1)S(1)} %bitcast.117, bf16[16,2]{0,1:T(2,128)(2,1)S(1)} %and_convert_fusion.7, pred[]{:T(512)S(6)} %compare.66), kind=kOutput, calls=%fused_computation.53.clone.clone.1 | convolution fusion | flops 1078460416 | bytes 6815937 | tf_op jit(solution)/shard_map/while/body/eval_jaxpr/nrxy,njyz->rjxz/dot_general | solution.py:93
  239.0 0.4 select_reduce_fusion.7
  239.6 7.2 %gather_fusion.1 = bf16[128,128,128]{2,1,0:T(8,128)(2,1)} fusion(bf16[337,128,128]{2,1,0:T(8,128)(2,1)} %get-tuple-element.963, s32[1024]{0:T(1024)S(1)} %pad_clamp_fusion.9), kind=kCustom, calls=%fused_computation.2.clone.clone.clone.1 | custom fusion | bytes 8389120 | tf_op jit(solution)/shard_map/while/body/eval_jaxpr/jit(_take)/gather | solution.py:88
  246.9 4.8 %fusion.105 = f32[8,2,128,128]{2,3,0,1:T(8,128)} fusion(bf16[16,8,128,128]{3,2,1,0:T(8,128)(2,1)} %bitcast.114, pred[16,8]{0,1:T(8,128)(4,1)S(1)} %copy.108, f32[8,2,128,128]{2,3,0,1:T(8,128)} %get-tuple-element.945, bf16[16,128,128]{1,2,0:T(8,128)(2,1)S(1)} %bitcast.117, bf16[16,2]{0,1:T(2,128)(2,1)S(1)} %and_convert_fusion.7, pred[]{:T(512)S(6)} %compare.66), kind=kOutput, calls=%fused_computation.53.clone.clone.1 | convolution fusion | flops 1078460416 | bytes 6815937 | tf_op jit(solution)/shard_map/while/body/eval_jaxpr/nrxy,njyz->rjxz/dot_general | solution.py:93
  251.7 1.6 copy.72
  253.3 0.6 gather_fusion.4
  253.8 0.7 fusion.54
  (210 shorter events, 10.9 us)
Async XLA Ops:
  0.6 34.0 %copy-start = (s32[8,32,2]{1,2,0:T(2,128)S(1)}, s32[8,32,2]{1,2,0:T(2,128)}, u32[]{:S(2)}) copy-start(s32[8,32,2]{1,2,0:T(2,128)} %param.16) | copy-start | bytes 6148
  0.6 33.6 %copy-start.6 = (s32[8,32]{1,0:T(8,128)S(1)}, s32[8,32]{1,0:T(8,128)}, u32[]{:S(2)}) copy-start(s32[8,32]{1,0:T(8,128)} %param.15) | copy-start | bytes 3076
  0.7 16.1 %collective-permute-start = (bf16[1,1,42,128,128]{4,3,2,1,0:T(8,128)(2,1)}, bf16[1,1,42,128,128]{4,3,2,1,0:T(8,128)(2,1)S(1)}, u32[]{:S(2)}, u32[]{:S(2)}) collective-permute-start(bf16[1,1,42,128,128]{4,3,2,1,0:T(8,128)(2,1)} %param.13), channel_id=1, source_target_pairs={{0,32},{32,64},{64,96},{96,128},{128,160},{160,192},{192,224},{224... | collective-permute-start | bytes 4128776 | tf_op jit(solution)/shard_map/ppermute | solution.py:22
  1.2 36.9 %collective-permute-start.1 = (bf16[1,1,42,128,128]{4,3,2,1,0:T(8,128)(2,1)}, bf16[1,1,42,128,128]{4,3,2,1,0:T(8,128)(2,1)}, u32[]{:S(2)}, u32[]{:S(2)}) collective-permute-start(bf16[1,1,42,128,128]{4,3,2,1,0:T(8,128)(2,1)} %param.13), channel_id=1, source_target_pairs={{0,224},{32,0},{64,32},{96,64},{128,96},{160,128},{192,160},{224,1... | collective-permute-start | bytes 4128776 | tf_op jit(solution)/shard_map/ppermute | solution.py:27
  16.7 26.4 %copy-start.2 = (bf16[1,1,42,128,128]{4,3,2,1,0:T(8,128)(2,1)}, bf16[1,1,42,128,128]{4,3,2,1,0:T(8,128)(2,1)S(1)}, u32[]{:S(2)}) copy-start(bf16[1,1,42,128,128]{4,3,2,1,0:T(8,128)(2,1)S(1)} %collective-permute-done) | copy-start | bytes 4128772
  16.7 22.1 %collective-permute-start.2 = (bf16[1,1,42,128,128]{4,3,2,1,0:T(8,128)(2,1)S(1)}, bf16[1,1,42,128,128]{4,3,2,1,0:T(8,128)(2,1)}, u32[]{:S(2)}, u32[]{:S(2)}) collective-permute-start(bf16[1,1,42,128,128]{4,3,2,1,0:T(8,128)(2,1)S(1)} %collective-permute-done), channel_id=1, source_target_pairs={{0,32},{32,64},{64,96},{96,128},{128,160},{160,192},{192,224},{224... | collective-permute-start | bytes 4128776 | tf_op jit(solution)/shard_map/ppermute | solution.py:22
  23.1 61.1 %all-to-all-start = ((bf16[32,1,1,2,128,128]{4,5,3,2,1,0:T(8,128)(2,1)}), bf16[32,1,1,2,128,128]{4,5,3,2,1,0:T(8,128)(2,1)}, u32[]{:S(2)}, u32[]{:S(2)}) async-start(bf16[32,1,1,2,128,128]{4,5,3,2,1,0:T(8,128)(2,1)} %broadcast_in_dim.202), calls=%async_computation | async-start | bytes 4194304 | tf_op jit(solution)/shard_map/all_to_all | solution.py:43
  38.1 19.6 %collective-permute-start.3 = (bf16[1,1,42,128,128]{4,3,2,1,0:T(8,128)(2,1)}, bf16[1,1,42,128,128]{4,3,2,1,0:T(8,128)(2,1)}, u32[]{:S(2)}, u32[]{:S(2)}) collective-permute-start(bf16[1,1,42,128,128]{4,3,2,1,0:T(8,128)(2,1)} %collective-permute-done.1), channel_id=1, source_target_pairs={{0,224},{32,0},{64,32},{96,64},{128,96},{160,128},{192,160},{224,1... | collective-permute-start | bytes 4128776 | tf_op jit(solution)/shard_map/ppermute | solution.py:27
  38.8 7.1 %copy-start.4 = (s32[8,42]{1,0:T(8,128)}, s32[8,42]{1,0:T(8,128)S(1)}, u32[]{:S(2)}) copy-start(s32[8,42]{1,0:T(8,128)S(1)} %fusion.57) | copy-start | bytes 4036
  38.9 20.4 %collective-permute-start.4 = (bf16[1,1,42,128,128]{4,3,2,1,0:T(8,128)(2,1)}, bf16[1,1,42,128,128]{4,3,2,1,0:T(8,128)(2,1)}, u32[]{:S(2)}, u32[]{:S(2)}) collective-permute-start(bf16[1,1,42,128,128]{4,3,2,1,0:T(8,128)(2,1)} %collective-permute-done.2), channel_id=1, source_target_pairs={{0,32},{32,64},{64,96},{96,128},{128,160},{160,192},{192,224},{224... | collective-permute-start | bytes 4128776 | tf_op jit(solution)/shard_map/ppermute | solution.py:22
  43.2 2.8 %copy-start.1 = (bf16[1,1,42,128,128]{4,3,2,1,0:T(8,128)(2,1)S(1)}, bf16[1,1,42,128,128]{4,3,2,1,0:T(8,128)(2,1)}, u32[]{:S(2)}) copy-start(bf16[1,1,42,128,128]{4,3,2,1,0:T(8,128)(2,1)} %param.13) | copy-start | bytes 4128772
  57.7 19.6 %collective-permute-start.5 = (bf16[1,1,42,128,128]{4,3,2,1,0:T(8,128)(2,1)}, bf16[1,1,42,128,128]{4,3,2,1,0:T(8,128)(2,1)S(1)}, u32[]{:S(2)}, u32[]{:S(2)}) collective-permute-start(bf16[1,1,42,128,128]{4,3,2,1,0:T(8,128)(2,1)} %collective-permute-done.3), channel_id=1, source_target_pairs={{0,224},{32,0},{64,32},{96,64},{128,96},{160,128},{192,160},{224,1... | collective-permute-start | bytes 4128776 | tf_op jit(solution)/shard_map/ppermute | solution.py:27
  59.3 18.5 %collective-permute-start.6 = (bf16[1,1,42,128,128]{4,3,2,1,0:T(8,128)(2,1)}, bf16[1,1,42,128,128]{4,3,2,1,0:T(8,128)(2,1)S(1)}, u32[]{:S(2)}, u32[]{:S(2)}) collective-permute-start(bf16[1,1,42,128,128]{4,3,2,1,0:T(8,128)(2,1)} %collective-permute-done.4), channel_id=1, source_target_pairs={{0,32},{32,64},{64,96},{96,128},{128,160},{160,192},{192,224},{224... | collective-permute-start | bytes 4128776 | tf_op jit(solution)/shard_map/ppermute | solution.py:22
  78.0 6.3 %copy-start.3 = (f32[8,2,128,128]{2,3,0,1:T(8,128)S(1)}, f32[8,2,128,128]{2,3,0,1:T(8,128)}, u32[]{:S(2)}) copy-start(f32[8,2,128,128]{2,3,0,1:T(8,128)} %custom-call) | copy-start | bytes 3145732
  136.2 11.1 %copy-start.5 = (s32[8,42]{1,0:T(8,128)S(1)}, s32[8,42]{1,0:T(8,128)}, u32[]{:S(2)}) copy-start(s32[8,42]{1,0:T(8,128)} %get-tuple-element.980) | copy-start | bytes 4036
  139.1 58.6 %all-to-all-start.1 = ((bf16[32,1,1,2,128,128]{4,5,3,2,1,0:T(8,128)(2,1)}), bf16[32,1,1,2,128,128]{4,5,3,2,1,0:T(8,128)(2,1)S(1)}, u32[]{:S(2)}, u32[]{:S(2)}) async-start(bf16[32,1,1,2,128,128]{4,5,3,2,1,0:T(8,128)(2,1)} %broadcast_in_dim.211), calls=%async_computation.1 | async-start | bytes 4194304 | tf_op jit(solution)/shard_map/all_to_all | solution.py:43
